TPU v7x, 32 devices: a whole 2x2x4 slice. The times are simulated.
32 devices in a mesh: slab: 4 (over y, x), blk: 8 (over z, core).
Axes of the slice: x: 2, y: 2, z: 4, core: 2. Of those that a mesh axis runs over, the one named last changes fastest.
Arguments:
- amplitudes: bfloat16 [32, 3, 56, 128, 128], P('slab', None, 'blk'), may hold values from -6 to 6
- integrals: bfloat16 [32, 3, 1200, 1200], P(('slab', 'blk')), may hold values from -0.03125 to 0.03125
- slot_tile: int32 [56], replicated, may hold values from -1 to 99, as said below
Outputs:
- residual: float32 [3, 56, 128, 128], P(None, 'blk', 'slab')
Inputs may be any that keep to these rules, and one draw needn't show every extreme that they name: `slot_tile`: each of the 55 block pairs x * 10 + y with x <= y is named by exactly one slot; every other slot holds -1.
All inputs are finite; a program needn't handle non-finite values.
Results may differ from a plain program's by a relative error of at most 0.0003.
Values may be sent and summed in bfloat16 or wider, within the bound.
A program may use at most 128 MiB of HBM per device.

v0:
```python
import jax
import jax.numpy as jnp
from jax import lax
from jax.sharding import PartitionSpec as P


def strict_upper(tile_len):
    row_ids = jnp.arange(tile_len)[:, None]
    col_ids = jnp.arange(tile_len)[None, :]
    return row_ids < col_ids


def local(amplitudes, integrals, slot_tile):
    moved = lax.all_to_all(amplitudes, "blk", split_axis=0, concat_axis=2, tiled=True)
    n_out = moved.shape[1]
    n_slots = moved.shape[2]
    tile_len = moved.shape[3]
    v_width = integrals.shape[-1]
    blocks = (v_width + tile_len - 1) // tile_len
    padded_len = blocks * tile_len
    tile_ids = jnp.arange(blocks * blocks, dtype=jnp.int32)
    matches = tile_ids[:, None] == slot_tile[None, :]
    on_diag = jnp.logical_and(slot_tile >= 0, slot_tile // blocks == slot_tile % blocks)
    keeping = jnp.logical_or(jnp.logical_not(on_diag)[:, None, None], strict_upper(tile_len)[None])
    selector = matches.astype(jnp.bfloat16)
    row_keep = (jnp.arange(padded_len) < v_width).astype(jnp.float32).reshape(blocks, tile_len, 1)
    padded_ints = jnp.pad(
        integrals, ((0, 0), (0, 0), (0, padded_len - v_width), (0, padded_len - v_width))
    )

    def unpack_tiles(packed):
        masked = jnp.where(keeping, packed, jnp.zeros((), packed.dtype)).reshape(
            n_slots, tile_len * tile_len
        )
        tiles = jnp.dot(selector, masked, preferred_element_type=jnp.float32).astype(jnp.bfloat16)
        tiles = tiles.reshape(blocks, blocks, tile_len, tile_len)
        return tiles - tiles.transpose(1, 0, 3, 2)

    ordered = [
        (source, target) for source in range(n_out) for target in range(n_out) if source != target
    ]
    sums = {pair: jnp.zeros((blocks, tile_len, padded_len), jnp.float32) for pair in ordered}
    fulls = [unpack_tiles(moved[0, source]) for source in range(n_out)]
    for pair in ordered:
        rows_w = padded_ints[0, pair[1]].reshape(blocks, tile_len, padded_len)
        product = jnp.einsum(
            "xyac,ycb->xab", fulls[pair[0]], rows_w, preferred_element_type=jnp.float32
        )
        sums[pair] = product * row_keep
    safe_ids = jnp.clip(slot_tile, 0, blocks * blocks - 1)
    first_blk = safe_ids // blocks
    second_blk = safe_ids % blocks
    present = (slot_tile >= 0)[:, None, None]
    packed_list = []
    for source in range(n_out):
        for target in range(source + 1, n_out):
            differ = (sums[source, target] - sums[target, source]).reshape(
                blocks, tile_len, blocks, tile_len
            )
            direct = differ[first_blk, :, second_blk, :]
            mirror = differ[second_blk, :, first_blk, :]
            tiled = direct - jnp.swapaxes(mirror, 1, 2)
            packed_list.append(jnp.where(present, tiled, jnp.zeros((), jnp.float32)))
    packed = jnp.stack(packed_list)
    n_pair = packed.shape[0]
    n_slab = lax.axis_size("slab")
    n_blk = lax.axis_size("blk")
    row_part = tile_len // n_slab
    slot_dev = n_slots // n_blk
    arranged = packed.reshape(n_pair, n_blk, slot_dev, n_slab, row_part, tile_len)
    arranged = arranged.transpose(3, 1, 0, 2, 4, 5).reshape(
        n_slab * n_blk, n_pair, slot_dev, row_part, tile_len
    )
    shares = lax.psum_scatter(arranged, ("slab", "blk"), scatter_dimension=0, tiled=True)
    return shares.reshape(n_pair, slot_dev, row_part, tile_len)


def solution(mesh):
    return jax.shard_map(
        local,
        mesh=mesh,
        in_specs=(P("slab", None, "blk", None, None), P(("slab", "blk"), None, None, None), P()),
        out_specs=P(None, "blk", "slab", None),
        check_vma=False,
    )
```

profile of v0, /device:TPU:0, one launch (start us, length us, event | category | flops | bytes accessed | tf_op | source)
XLA Modules:
  0.0 492.8 jit_solution(1825716892702521608)
XLA Ops:
  6.5 6.5 %all-to-all-start = ((bf16[8,3,7,128,128]{4,3,2,1,0:T(8,128)(2,1)}), bf16[8,3,7,128,128]{4,3,2,1,0:T(8,128)(2,1)}, u32[]{:S(2)}, u32[]{:S(2)}) async-start(bf16[8,3,7,128,128]{4,3,2,1,0:T(8,128)(2,1)} %param.3), calls=%async_computation | async-start | bytes 11010048 | tf_op jit(solution)/shard_map/all_to_all | solution.py:14
  13.2 6.5 %pad_slice_fusion.1 = (bf16[1,1,1280,1280]{3,2,1,0:T(8,128)(2,1)}, bf16[1,1,1280,1280]{3,2,1,0:T(8,128)(2,1)}, bf16[1,1,1280,1280]{3,2,1,0:T(8,128)(2,1)}) fusion(bf16[1,3,1200,1200]{3,2,1,0:T(8,128)(2,1)} %param.4), kind=kLoop, calls=%fused_computation.11 | loop fusion | bytes 18470400 | tf_op jit(solution)/shard_map/slice | solution.py:45
  19.7 115.5 %all-to-all-done = bf16[8,3,7,128,128]{4,3,2,1,0:T(8,128)(2,1)} async-done(((bf16[8,3,7,128,128]{4,3,2,1,0:T(8,128)(2,1)}), bf16[8,3,7,128,128]{4,3,2,1,0:T(8,128)(2,1)}, u32[]{:S(2)}, u32[]{:S(2)}) %all-to-all-start) | async-done | bytes 5505056 | tf_op jit(solution)/shard_map/all_to_all | solution.py:14
  135.2 3.7 copy.43
  144.9 3.5 copy.44
  154.6 5.6 %copy.45 = bf16[10,10,128,128]{2,3,0,1:T(8,128)(2,1)} copy(bf16[10,10,128,128]{3,2,1,0:T(8,128)(2,1)} %bitcast.139) | data formatting | bytes 6553600 | tf_op jit(solution)/shard_map/reshape | solution.py:36
  160.3 7.7 %fusion.19 = f32[10,128,1280,1]{2,1,3,0:T(8,128)S(1)} fusion(bf16[10,128,1280,1]{2,1,0,3:T(8,128)(2,1)} %bitcast.149, bf16[10,10,128,128]{3,2,1,0:T(8,128)(2,1)S(1)} %bitcast.134, bf16[10,10,128,128]{2,3,0,1:T(8,128)(2,1)} %copy.44), kind=kOutput, calls=%fused_computation.47 | convolution fusion | flops 4195942400 | bytes 16384000 | tf_op jit(solution)/shard_map/xyac,ycb->xab/dot_general | solution.py:46
  168.0 6.8 %fusion.2 = f32[10,128,1280]{2,1,0:T(8,128)} fusion(f32[10,128,1280,1]{2,1,3,0:T(8,128)S(1)} %fusion.19, bf16[10,128,1280,1]{2,1,0,3:T(8,128)(2,1)S(1)} %bitcast.145, f32[10,128]{1,0:T(8,128)S(1)} %fusion.28, bf16[10,10,128,128]{3,2,1,0:T(8,128)(2,1)S(1)} %bitcast.141, bf16[10,10,128,128]{2,3,0,1:T(8,128)(2,1)S(1)} %copy-done.4), kind=kOutput, calls=%fused_computation.20 | convolution fusion | flops 4200857600 | bytes 22942720 | tf_op jit(solution)/shard_map/xyac,ycb->xab/dot_general | solution.py:46
  174.7 8.2 %copy.46 = f32[10,128,1280]{1,2,0:T(8,128)} copy(f32[10,128,1280]{2,1,0:T(8,128)} %fusion.2) | data formatting | bytes 13107200 | tf_op jit(solution)/shard_map/sub | solution.py:57
  182.9 8.2 %copy.47 = f32[10,128,10,128]{3,1,2,0:T(8,128)} copy(f32[10,128,10,128]{1,3,2,0:T(8,128)} %bitcast.120) | data formatting | bytes 13107200 | tf_op jit(solution)/shard_map/reshape | solution.py:57
  191.1 5.5 %gather_fusion = f32[56,128,128]{2,1,0:T(8,128)} fusion(f32[10,128,10,128]{3,1,2,0:T(8,128)} %copy.47, s32[56]{0:T(128)S(1)} %shift-left_or_fusion.1), kind=kCustom, calls=%fused_computation | custom fusion | bytes 7340480 | tf_op jit(solution)/shard_map/gather | solution.py:60
  196.6 5.5 %gather_fusion.1 = f32[56,128,128]{2,1,0:T(8,128)} fusion(f32[10,128,10,128]{3,1,2,0:T(8,128)} %copy.47, s32[56]{0:T(128)S(1)} %get-tuple-element.5), kind=kCustom, calls=%fused_computation.1 | custom fusion | bytes 7340480 | tf_op jit(solution)/shard_map/gather | solution.py:61
  202.1 9.5 %fusion.20 = f32[10,128,1280,1]{2,1,3,0:T(8,128)} fusion(bf16[10,128,1280,1]{2,1,0,3:T(8,128)(2,1)} %bitcast.147, bf16[10,10,128,128]{3,2,1,0:T(8,128)(2,1)} %bitcast.140, bf16[10,10,128,128]{2,3,0,1:T(8,128)(2,1)} %copy.45), kind=kOutput, calls=%fused_computation.48 | convolution fusion | flops 4195942400 | bytes 16384000 | tf_op jit(solution)/shard_map/xyac,ycb->xab/dot_general | solution.py:46
  216.3 5.6 %copy.50 = bf16[10,10,128,128]{2,3,0,1:T(8,128)(2,1)} copy(bf16[10,10,128,128]{3,2,1,0:T(8,128)(2,1)} %bitcast.136) | data formatting | bytes 6553600 | tf_op jit(solution)/shard_map/reshape | solution.py:36
  221.9 10.4 %fusion = f32[10,128,1280]{2,1,0:T(8,128)} fusion(f32[10,128,1280,1]{2,1,3,0:T(8,128)} %fusion.20, bf16[10,128,1280,1]{2,1,0,3:T(8,128)(2,1)} %bitcast.150, f32[10,128]{1,0:T(8,128)S(1)} %fusion.28, bf16[10,10,128,128]{3,2,1,0:T(8,128)(2,1)} %bitcast.137, bf16[10,10,128,128]{2,3,0,1:T(8,128)(2,1)} %copy.50), kind=kOutput, calls=%fused_computation.14 | convolution fusion | flops 4200857600 | bytes 22942720 | tf_op jit(solution)/shard_map/xyac,ycb->xab/dot_general | solution.py:46
  232.3 8.2 %copy.55 = f32[10,128,1280]{1,2,0:T(8,128)} copy(f32[10,128,1280]{2,1,0:T(8,128)} %fusion) | data formatting | bytes 13107200 | tf_op jit(solution)/shard_map/sub | solution.py:57
  240.5 8.2 %copy.56 = f32[10,128,10,128]{3,1,2,0:T(8,128)} copy(f32[10,128,10,128]{1,3,2,0:T(8,128)} %bitcast.121) | data formatting | bytes 13107200 | tf_op jit(solution)/shard_map/reshape | solution.py:57
  248.6 5.6 %gather_fusion.4 = f32[56,128,128]{2,1,0:T(8,128)} fusion(f32[10,128,10,128]{3,1,2,0:T(8,128)} %copy.56, s32[56]{0:T(128)S(1)} %shift-left_or_fusion.1), kind=kCustom, calls=%fused_computation.4 | custom fusion | bytes 7340480 | tf_op jit(solution)/shard_map/gather | solution.py:60
  254.2 5.6 %gather_fusion.5 = f32[56,128,128]{2,1,0:T(8,128)} fusion(f32[10,128,10,128]{3,1,2,0:T(8,128)} %copy.56, s32[56]{0:T(128)S(1)} %get-tuple-element.5), kind=kCustom, calls=%fused_computation.5 | custom fusion | bytes 7340480 | tf_op jit(solution)/shard_map/gather | solution.py:61
  259.8 7.7 %fusion.18 = f32[10,128,1280,1]{2,1,3,0:T(8,128)S(1)} fusion(bf16[10,128,1280,1]{2,1,0,3:T(8,128)(2,1)} %bitcast.148, bf16[10,10,128,128]{3,2,1,0:T(8,128)(2,1)S(1)} %bitcast.135, bf16[10,10,128,128]{2,3,0,1:T(8,128)(2,1)} %copy.44), kind=kOutput, calls=%fused_computation.46 | convolution fusion | flops 4195942400 | bytes 16384000 | tf_op jit(solution)/shard_map/xyac,ycb->xab/dot_general | solution.py:46
  267.5 6.6 %fusion.1 = f32[10,128,1280]{2,1,0:T(8,128)} fusion(f32[10,128,1280,1]{2,1,3,0:T(8,128)S(1)} %fusion.18, bf16[10,128,1280,1]{2,1,0,3:T(8,128)(2,1)S(1)} %bitcast.146, f32[10,128]{1,0:T(8,128)S(1)} %fusion.28, bf16[10,10,128,128]{3,2,1,0:T(8,128)(2,1)S(1)} %bitcast.138, bf16[10,10,128,128]{2,3,0,1:T(8,128)(2,1)S(1)} %copy-done.3), kind=kOutput, calls=%fused_computation.17 | convolution fusion | flops 4200857600 | bytes 22942720 | tf_op jit(solution)/shard_map/xyac,ycb->xab/dot_general | solution.py:46
  274.1 8.2 %copy.51 = f32[10,128,1280]{1,2,0:T(8,128)} copy(f32[10,128,1280]{2,1,0:T(8,128)} %fusion.1) | data formatting | bytes 13107200 | tf_op jit(solution)/shard_map/sub | solution.py:57
  282.3 8.2 %copy.52 = f32[10,128,10,128]{3,1,2,0:T(8,128)} copy(f32[10,128,10,128]{1,3,2,0:T(8,128)} %bitcast.122) | data formatting | bytes 13107200 | tf_op jit(solution)/shard_map/reshape | solution.py:57
  290.4 5.6 %gather_fusion.2 = f32[56,128,128]{2,1,0:T(8,128)} fusion(f32[10,128,10,128]{3,1,2,0:T(8,128)} %copy.52, s32[56]{0:T(128)S(1)} %shift-left_or_fusion.1), kind=kCustom, calls=%fused_computation.2 | custom fusion | bytes 7340480 | tf_op jit(solution)/shard_map/gather | solution.py:60
  296.0 5.5 %gather_fusion.3 = f32[56,128,128]{2,1,0:T(8,128)} fusion(f32[10,128,10,128]{3,1,2,0:T(8,128)} %copy.52, s32[56]{0:T(128)S(1)} %get-tuple-element.5), kind=kCustom, calls=%fused_computation.3 | custom fusion | bytes 7340480 | tf_op jit(solution)/shard_map/gather | solution.py:61
  301.6 5.2 %copy.49 = f32[56,128,128]{1,2,0:T(8,128)} copy(f32[56,128,128]{2,1,0:T(8,128)} %gather_fusion.1) | data formatting | bytes 7340032 | tf_op jit(solution)/shard_map/gather | solution.py:61
  306.8 5.3 %copy.58 = f32[56,128,128]{1,2,0:T(8,128)} copy(f32[56,128,128]{2,1,0:T(8,128)} %gather_fusion.5) | data formatting | bytes 7340032 | tf_op jit(solution)/shard_map/gather | solution.py:61
  312.1 5.3 %copy.54 = f32[56,128,128]{1,2,0:T(8,128)} copy(f32[56,128,128]{2,1,0:T(8,128)} %gather_fusion.3) | data formatting | bytes 7340032 | tf_op jit(solution)/shard_map/gather | solution.py:61
  317.3 12.8 %fusion.5 = (f32[56,128,128]{2,1,0:T(8,128)}, f32[56,128,128]{2,1,0:T(8,128)}, f32[56,128,128]{2,1,0:T(8,128)}) fusion(f32[56,128,128]{2,1,0:T(8,128)} %gather_fusion, f32[56,128,128]{1,2,0:T(8,128)} %copy.49, pred[56]{0:T(512)(128)(4,1)S(1)} %get-tuple-element.17, f32[56,128,128]{2,1,0:T(8,128)} %gather_fusion.4, f32[56,128,128]{1,2,0:T(8,128)} %copy.58, ...), kind=kLoop, calls=%fused_computation.30 | loop fusion | flops 5505024 | bytes 33030200 | tf_op jit(solution)/shard_map/jit(_where)/select_n | solution.py:63
  330.1 6.7 %maximum_bitcast_fusion = f32[4,8,3,7,32,128]{5,4,0,3,1,2:T(8,128)S(1)} fusion(f32[1,8,7,4,32,128]{5,4,3,2,1,0:T(8,128)} %bitcast.125, f32[1,8,7,4,32,128]{5,4,3,2,1,0:T(8,128)} %bitcast.126, f32[1,8,7,4,32,128]{5,4,3,2,1,0:T(8,128)} %bitcast.124), kind=kLoop, calls=%fused_computation.9 | loop fusion | flops 5505024 | bytes 22020096 | tf_op jit(solution)/shard_map/transpose | solution.py:71
  336.9 6.0 %copy.59 = f32[4,8,3,7,32,128]{5,4,3,2,1,0:T(8,128)} copy(f32[4,8,3,7,32,128]{5,4,0,3,1,2:T(8,128)S(1)} %maximum_bitcast_fusion) | data formatting | bytes 22020096 | tf_op jit(solution)/shard_map/transpose | solution.py:71
  342.9 143.1 %reduce-scatter.2.cloned.1.call-done = f32[1,3,7,32,128]{4,3,2,1,0:T(8,128)} async-done(((f32[32,3,7,32,128]{4,3,2,1,0:T(8,128)}), f32[1,3,7,32,128]{4,3,2,1,0:T(8,128)}) %reduce-scatter.2.cloned.1.call-update) | async-done | bytes 344080 | tf_op jit(solution)/shard_map/reduce_scatter | solution.py:74
  (33 shorter events, 17.0 us)
Async XLA Ops:
  6.5 6.5 %copy-start.7 = (s32[56]{0:T(128)S(1)}, s32[56]{0:T(128)}, u32[]{:S(2)}) copy-start(s32[56]{0:T(128)} %param.5) | copy-start | bytes 676
  6.5 128.7 %all-to-all-start = ((bf16[8,3,7,128,128]{4,3,2,1,0:T(8,128)(2,1)}), bf16[8,3,7,128,128]{4,3,2,1,0:T(8,128)(2,1)}, u32[]{:S(2)}, u32[]{:S(2)}) async-start(bf16[8,3,7,128,128]{4,3,2,1,0:T(8,128)(2,1)} %param.3), calls=%async_computation | async-start | bytes 11010048 | tf_op jit(solution)/shard_map/all_to_all | solution.py:14
  13.0 473.0 %reduce-scatter.2.cloned.1.call-start = ((), (), s32[]{:S(2)}) async-start(), calls=%async_computation.2 | async-start | bytes 11354112 | tf_op jit(solution)/shard_map/reduce_scatter | solution.py:74
  160.3 7.7 %copy-start.1 = (bf16[100,128,128]{2,1,0:T(8,128)(2,1)S(1)}, bf16[100,128,128]{2,1,0:T(8,128)(2,1)}, u32[]{:S(2)}) copy-start(bf16[100,128,128]{2,1,0:T(8,128)(2,1)} %slice.43) | copy-start | bytes 9830404
  160.3 7.7 %copy-start.4 = (bf16[10,10,128,128]{2,3,0,1:T(8,128)(2,1)S(1)}, bf16[10,10,128,128]{2,3,0,1:T(8,128)(2,1)}, u32[]{:S(2)}) copy-start(bf16[10,10,128,128]{2,3,0,1:T(8,128)(2,1)} %copy.45) | copy-start | bytes 9830404
  160.3 7.7 %copy-start.5 = (bf16[1,1,1280,1280]{3,2,1,0:T(8,128)(2,1)S(1)}, bf16[1,1,1280,1280]{3,2,1,0:T(8,128)(2,1)}, u32[]{:S(2)}) copy-start(bf16[1,1,1280,1280]{3,2,1,0:T(8,128)(2,1)} %get-tuple-element.8) | copy-start | bytes 9830404
  202.1 9.5 %copy-start.2 = (bf16[1,1,56,128,128]{4,3,2,1,0:T(8,128)(2,1)S(1)}, bf16[1,1,56,128,128]{4,3,2,1,0:T(8,128)(2,1)}, u32[]{:S(2)}) copy-start(bf16[1,1,56,128,128]{4,3,2,1,0:T(8,128)(2,1)} %get-tuple-element.12) | copy-start | bytes 5505028
  259.8 7.7 %copy-start = (bf16[100,128,128]{2,1,0:T(8,128)(2,1)S(1)}, bf16[100,128,128]{2,1,0:T(8,128)(2,1)}, u32[]{:S(2)}) copy-start(bf16[100,128,128]{2,1,0:T(8,128)(2,1)} %slice.44) | copy-start | bytes 9830404
  259.8 7.7 %copy-start.3 = (bf16[10,10,128,128]{2,3,0,1:T(8,128)(2,1)S(1)}, bf16[10,10,128,128]{2,3,0,1:T(8,128)(2,1)}, u32[]{:S(2)}) copy-start(bf16[10,10,128,128]{2,3,0,1:T(8,128)(2,1)} %copy.50) | copy-start | bytes 9830404
  259.8 7.7 %copy-start.6 = (bf16[1,1,1280,1280]{3,2,1,0:T(8,128)(2,1)S(1)}, bf16[1,1,1280,1280]{3,2,1,0:T(8,128)(2,1)}, u32[]{:S(2)}) copy-start(bf16[1,1,1280,1280]{3,2,1,0:T(8,128)(2,1)} %get-tuple-element.8) | copy-start | bytes 9830404
Sparse Core Ops, SparseCore 0:
  343.0 142.9 reduce-scatter.1
where the time goes:
time: 495 us; the launch traced here: 493 us
  waiting for transfers between devices  259 us (52%)
  local copies, waits for them, and re-layouts  139 us (28%)
  matrix products  55.4 us (11%)
  other arithmetic  19.6 us (4%)
  between operations  13.6 us (3%)
  starting transfers between devices  6.52 us (1%)
    reduce_scatter x1, waiting for transfers between devices, local(): lax.psum_scatter(arranged, ('slab', 'blk'), scatter_dimension=0, tiled=True)  143 us
    all_to_all x1, waiting for transfers between devices, local(): lax.all_to_all(amplitudes, 'blk', split_axis=0, concat_axis=2, tiled=True)  115 us
    dot_general x6, matrix products, local(): jnp.einsum('xyac,ycb->xab', fulls[pair[0]], rows_w, preferred_element_typ...  48.6 us
    gather x6, local copies, waits for them, and re-layouts, local(): mirror = differ[second_blk, :, first_blk, :]  32.4 us
    sub x3, local copies, waits for them, and re-layouts, local(): sums[source, target] - sums[target, source]  24.5 us
    reshape x3, local copies, waits for them, and re-layouts, local(): (sums[source, target] - sums[target, source]).reshape(blocks, tile_len, b...  24.5 us
    gather x3, local copies, waits for them, and re-layouts, local(): direct = differ[first_blk, :, second_blk, :]  16.6 us
    reshape x3, local copies, waits for them, and re-layouts, unpack_tiles(): tiles = tiles.reshape(blocks, blocks, tile_len, tile_len)  14.7 us
  transfers between devices with their start and end apart: 2, of which 2 were waited for; matrix products, arithmetic and copies ran while one was open for 1% of the time, Pallas kernels for 0%

commit v1 on v0

v1 whole, which is shorter than its diff:
```python
import functools

import jax
import jax.numpy as jnp
from jax import lax
from jax.experimental import pallas as pl
from jax.experimental.pallas import tpu as pltpu
from jax.sharding import PartitionSpec as P


def assemble_kernel(v_width, blocks, slot_ref, packed_ref, full_ref):
    n_slots, tile_len, _ = packed_ref.shape
    row_ids = lax.broadcasted_iota(jnp.int32, (tile_len, tile_len), 0)
    col_ids = lax.broadcasted_iota(jnp.int32, (tile_len, tile_len), 1)

    def place(slot, carry):
        tile_id = slot_ref[slot]

        @pl.when(tile_id >= 0)
        def _():
            first = lax.div(tile_id, blocks)
            second = lax.rem(tile_id, blocks)
            rows = pl.ds(pl.multiple_of(first * tile_len, tile_len), tile_len)
            cols = pl.ds(pl.multiple_of(second * tile_len, tile_len), tile_len)
            row_at = row_ids + first * tile_len
            col_at = col_ids + second * tile_len
            keep = jnp.logical_and(row_at < col_at, col_at < v_width)
            tile = jnp.where(keep, packed_ref[slot].astype(jnp.float32), 0.0)
            mirror = tile.T

            @pl.when(first == second)
            def _():
                full_ref[rows, cols] = (tile - mirror).astype(full_ref.dtype)

            @pl.when(first != second)
            def _():
                full_ref[rows, cols] = tile.astype(full_ref.dtype)
                full_ref[cols, rows] = (-mirror).astype(full_ref.dtype)

        return carry

    lax.fori_loop(0, n_slots, place, 0)


def assemble(slot_tile, packed, v_width, blocks):
    tile_len = packed.shape[-1]
    padded = blocks * tile_len
    return pl.pallas_call(
        functools.partial(assemble_kernel, v_width, blocks),
        out_shape=jax.ShapeDtypeStruct((padded, padded), packed.dtype),
        in_specs=[
            pl.BlockSpec(memory_space=pltpu.SMEM),
            pl.BlockSpec(memory_space=pltpu.VMEM),
        ],
        out_specs=pl.BlockSpec(memory_space=pltpu.VMEM),
        compiler_params=pltpu.CompilerParams(vmem_limit_bytes=24 << 20),
        cost_estimate=pl.CostEstimate(
            flops=0, bytes_accessed=4 * padded * padded, transcendentals=0
        ),
        name="assemble",
    )(slot_tile, packed)


def pair_kernel(
    blocks, n_slab, n_blk, slot_ref, left_ref, right_ref, wl_ref, wr_ref, out_ref, weights, differ
):
    padded = left_ref.shape[0]
    v_width = wl_ref.shape[-1]
    tile_len = padded // blocks
    row_part = tile_len // n_slab
    slot_dev = out_ref.shape[2]
    pad = padded - v_width
    for half, ref in enumerate((wr_ref, wl_ref)):
        base = half * padded
        vals = ref[0, 0]
        weights[pl.ds(base, v_width), pl.ds(0, v_width)] = vals if half == 0 else -vals
        if pad:
            weights[pl.ds(base, padded), pl.ds(v_width, pad)] = jnp.zeros((padded, pad), weights.dtype)
            weights[pl.ds(base + v_width, pad), :] = jnp.zeros((pad, padded), weights.dtype)

    width = 2 * tile_len if padded % (2 * tile_len) == 0 else tile_len

    def columns(step, carry):
        cols = pl.ds(pl.multiple_of(step * width, width), width)
        top = jnp.dot(left_ref[...], weights[pl.ds(0, padded), cols], preferred_element_type=jnp.float32)
        low = jnp.dot(right_ref[...], weights[pl.ds(padded, padded), cols], preferred_element_type=jnp.float32)
        differ[:, cols] = top + low
        return carry

    lax.fori_loop(0, padded // width, columns, 0)

    def pack(slot, carry):
        tile_id = slot_ref[slot]
        owner = lax.div(slot, slot_dev)
        place = lax.rem(slot, slot_dev)

        @pl.when(tile_id >= 0)
        def _():
            first = lax.div(tile_id, blocks)
            second = lax.rem(tile_id, blocks)
            rows = pl.ds(pl.multiple_of(first * tile_len, tile_len), tile_len)
            cols = pl.ds(pl.multiple_of(second * tile_len, tile_len), tile_len)
            tile = differ[rows, cols] - differ[cols, rows].T
            for slab in range(n_slab):
                part = tile[slab * row_part : (slab + 1) * row_part]
                out_ref[slab, owner, place] = part

        @pl.when(tile_id < 0)
        def _():
            for slab in range(n_slab):
                out_ref[slab, owner, place] = jnp.zeros((row_part, tile_len), jnp.float32)

        return carry

    lax.fori_loop(0, n_blk * slot_dev, pack, 0)


def pair_tiles(slot_tile, fulls, integrals, source, target, n_slab, n_blk, tile_len):
    padded = fulls[0].shape[0]
    blocks = padded // tile_len
    v_width = integrals.shape[-1]
    slot_dev = slot_tile.shape[0] // n_blk
    vmem = pl.BlockSpec(memory_space=pltpu.VMEM)

    def ints(which):
        return pl.BlockSpec((1, 1, v_width, v_width), lambda i: (0, which, 0, 0), pipeline_mode=pl.Buffered(1))

    def whole(shape):
        return pl.BlockSpec(shape, lambda i: (0,) * len(shape), pipeline_mode=pl.Buffered(1))

    out_dims = (n_slab, n_blk, slot_dev, tile_len // n_slab, tile_len)
    return pl.pallas_call(
        functools.partial(pair_kernel, blocks, n_slab, n_blk),
        grid=(1,),
        out_shape=jax.ShapeDtypeStruct(out_dims, jnp.float32),
        in_specs=[
            pl.BlockSpec(memory_space=pltpu.SMEM),
            whole((padded, padded)),
            whole((padded, padded)),
            ints(source),
            ints(target),
        ],
        out_specs=whole(out_dims),
        scratch_shapes=[
            pltpu.VMEM((2 * padded, padded), fulls[0].dtype),
            pltpu.VMEM((padded, padded), jnp.float32),
        ],
        compiler_params=pltpu.CompilerParams(vmem_limit_bytes=56 << 20),
        cost_estimate=pl.CostEstimate(
            flops=4 * padded * padded * padded, bytes_accessed=16 * padded * padded, transcendentals=0
        ),
        name="pair_tiles",
    )(slot_tile, fulls[source], fulls[target], integrals, integrals)


def local(amplitudes, integrals, slot_tile):
    n_slab = lax.axis_size("slab")
    n_blk = lax.axis_size("blk")
    n_out, slot_dev, tile_len = amplitudes.shape[1:4]
    v_width = integrals.shape[-1]
    blocks = (v_width + tile_len - 1) // tile_len
    n_slots = slot_tile.shape[0]
    fulls = []
    for source in range(n_out):
        moved = lax.all_to_all(
            amplitudes[:, source], "blk", split_axis=0, concat_axis=0, tiled=True
        )
        packed = moved.reshape(n_slots, tile_len, tile_len)
        fulls.append(assemble(slot_tile, packed, v_width, blocks))
    shares = []
    for target in range(n_out):
        for source in range(target):
            arranged = pair_tiles(
                slot_tile, fulls, integrals, source, target, n_slab, n_blk, tile_len
            )
            arranged = arranged.reshape(n_slab * n_blk, slot_dev, tile_len // n_slab, tile_len)
            share = lax.psum_scatter(arranged, ("slab", "blk"), scatter_dimension=0, tiled=True)
            shares.append((source, target, share))
    shares.sort(key=lambda item: item[:2])
    return jnp.concatenate([item[2] for item in shares])


def solution(mesh):
    return jax.shard_map(
        local,
        mesh=mesh,
        in_specs=(P("slab", None, "blk", None, None), P(("slab", "blk"), None, None, None), P()),
        out_specs=P(None, "blk", "slab", None),
        check_vma=False,
    )
```

time: 495 us -> 580 us (1.17)
  local copies, waits for them, and re-layouts: 139 us -> 14.4 us
  blocking collectives: 0 us -> 113 us
  Pallas kernels: 0 us -> 91.7 us
  waiting for transfers between devices: 259 us -> 342 us
  matrix products: 55.4 us -> 0 us
  other arithmetic: 19.6 us -> 1.76 us
    reduce_scatter x1 -> x3, waiting for transfers between devices: 143 us -> 309 us  [local(): lax.psum_scatter(arranged, ('slab', 'blk'), scatter_dimension=0, tiled=True)]
    all_to_all x0 -> x2, blocking collectives: none -> 113 us  [local(): lax.all_to_all(amplitudes[:, source], 'blk', split_axis=0, concat_axis=0,...]
    pallas_call x0 -> x6, Pallas kernels: none -> 91.7 us  [the longest x3 69.1 us: pair_tiles(): pl.pallas_call(functools.partial(pair_kernel, blocks, n_slab, n_blk), gri...]
    all_to_all x1, waiting for transfers between devices: 115 us -> 32.5 us  [local(): lax.all_to_all(amplitudes[:, source], 'blk', split_axis=0, concat_axis=0,...]
    dot_general x9 -> x0, matrix products: 55.4 us -> none  [the longest x6 48.6 us: local(): jnp.einsum('xyac,ycb->xab', fulls[pair[0]], rows_w, preferred_element_typ...]
    gather x9 -> x0, local copies, waits for them, and re-layouts: 49.1 us -> none  [the longest x6 32.4 us: local(): mirror = differ[second_blk, :, first_blk, :]]
    reshape x6 -> x0, local copies, waits for them, and re-layouts: 39.2 us -> none  [the longest x3 24.5 us: local(): (sums[source, target] - sums[target, source]).reshape(blocks, tile_len, b...]
    sub x3 -> x0, local copies, waits for them, and re-layouts: 24.5 us -> none  [local(): sums[source, target] - sums[target, source]]
  transfers between devices with their start and end apart: 2 -> 4, of which waited for: 2 -> 4; matrix products, arithmetic and copies ran while one was open for 1% -> 0% of each run, Pallas kernels for 0% -> 11%
where the time goes in v1:
time: 580 us; the launch traced here: 579 us
  waiting for transfers between devices  342 us (59%)
  blocking collectives  113 us (19%)
  Pallas kernels  91.7 us (16%)
  local copies, waits for them, and re-layouts  14.4 us (2%)
  between operations  13.2 us (2%)
    reduce_scatter x3, waiting for transfers between devices, local(): lax.psum_scatter(arranged, ('slab', 'blk'), scatter_dimension=0, tiled=True)  309 us
    all_to_all x2, blocking collectives, local(): lax.all_to_all(amplitudes[:, source], 'blk', split_axis=0, concat_axis=0,...  113 us
    pallas_call x3, Pallas kernels, pair_tiles(): pl.pallas_call(functools.partial(pair_kernel, blocks, n_slab, n_blk), gri...  69.1 us
    all_to_all x1, waiting for transfers between devices, local(): lax.all_to_all(amplitudes[:, source], 'blk', split_axis=0, concat_axis=0,...  32.5 us
    pallas_call x3, Pallas kernels, assemble(): pl.pallas_call(functools.partial(assemble_kernel, v_width, blocks), out_s...  22.6 us
  transfers between devices with their start and end apart: 4, of which 4 were waited for; matrix products, arithmetic and copies ran while one was open for 0% of the time, Pallas kernels for 11%

profile of v1, /device:TPU:0, one launch (start us, length us, event | category | flops | bytes accessed | tf_op | source)
XLA Modules:
  0.0 579.3 jit_solution(14890052906308473941)
XLA Ops:
  6.5 6.3 %slice_bitcast_fusion.2 = (bf16[8,7,128,128]{3,2,1,0:T(8,128)(2,1)S(1)}, bf16[8,7,128,128]{3,2,1,0:T(8,128)(2,1)}, bf16[8,7,128,128]{3,2,1,0:T(8,128)(2,1)}) fusion(bf16[8,3,7,128,128]{4,3,2,1,0:T(8,128)(2,1)} %param.3), kind=kLoop, calls=%fused_computation.2 | loop fusion | bytes 11010048 | tf_op jit(solution)/shard_map/squeeze | solution.py:166
  12.8 49.8 %all_to_all.15 = bf16[8,7,128,128]{3,2,1,0:T(8,128)(2,1)} all-to-all(bf16[8,7,128,128]{3,2,1,0:T(8,128)(2,1)S(1)} %get-tuple-element.5), channel_id=1, replica_groups=mesh['slab'=4,'blk'=8] {'blk'}, dimensions={0} | all-to-all | bytes 3670016 | tf_op jit(solution)/shard_map/all_to_all | solution.py:165
  62.6 3.6 all-to-all-start.1
  66.2 0.0 reduce-scatter.4.cloned.1.call-start
  66.3 0.0 copy-done.4
  66.3 0.0 copy-start
  66.3 1.5 copy-done
  67.8 7.5 %assemble.3.left_ref = bf16[1280,1280]{1,0:T(8,128)(2,1)S(1)} custom-call(s32[56]{0:T(128)S(1)} %copy-done.4, bf16[56,128,128]{2,1,0:T(8,128)(2,1)S(1)} %bitcast.13), custom_call_target="tpu_custom_call" | custom-call | bytes 6553600 | tf_op jit(solution)/shard_map/assemble/pallas_call | solution.py:48
  75.3 0.0 copy-start.2
  75.3 1.8 copy-done.2
  77.1 32.5 %all-to-all-done.1 = bf16[8,7,128,128]{3,2,1,0:T(8,128)(2,1)S(1)} async-done(((bf16[8,7,128,128]{3,2,1,0:T(8,128)(2,1)}), bf16[8,7,128,128]{3,2,1,0:T(8,128)(2,1)S(1)}, u32[]{:S(2)}, u32[]{:S(2)}) %all-to-all-start.1) | async-done | bytes 1835040 | tf_op jit(solution)/shard_map/all_to_all | solution.py:165
  109.6 7.5 %assemble.4.right_ref.left_ref = bf16[1280,1280]{1,0:T(8,128)(2,1)S(1)} custom-call(s32[56]{0:T(128)S(1)} %copy-done.4, bf16[56,128,128]{2,1,0:T(8,128)(2,1)S(1)} %bitcast.12), custom_call_target="tpu_custom_call" | custom-call | bytes 6553600 | tf_op jit(solution)/shard_map/assemble/pallas_call | solution.py:48
  117.1 0.0 copy-start.1
  117.1 1.8 copy-done.1
  118.9 23.0 %pair_tiles.3 = f32[4,8,7,32,128]{4,3,2,1,0:T(8,128)} custom-call(s32[56]{0:T(128)} %slot_ref.11, bf16[1280,1280]{1,0:T(8,128)(2,1)} %copy-done.2, bf16[1280,1280]{1,0:T(8,128)(2,1)} %copy-done.1, bf16[1,3,1200,1200]{3,2,1,0:T(8,128)(2,1)} %wr_ref.5, bf16[1,3,1200,1200]{3,2,1,0:T(8,128)(2,1)} %wr_ref.5), custom_call_target="tpu_custom_call" | custom-call | flops 8388608000 | bytes 26214400 | tf_op jit(solution)/shard_map/pair_tiles/pallas_call | solution.py:132
  141.9 0.0 reduce-scatter.4.cloned.1.call-update
  141.9 0.0 reduce-scatter.6.cloned.1.call-start
  141.9 1.4 copy-done.6
  143.4 62.9 %all_to_all.16 = bf16[8,7,128,128]{3,2,1,0:T(8,128)(2,1)S(1)} all-to-all(bf16[8,7,128,128]{3,2,1,0:T(8,128)(2,1)S(1)} %copy-done.6), channel_id=1, replica_groups=mesh['slab'=4,'blk'=8] {'blk'}, dimensions={0} | all-to-all | bytes 3670016 | tf_op jit(solution)/shard_map/all_to_all | solution.py:165
  206.3 0.0 copy-done.5
  206.3 7.5 %assemble.5.right_ref = bf16[1280,1280]{1,0:T(8,128)(2,1)S(1)} custom-call(s32[56]{0:T(128)S(1)} %copy-done.5, bf16[56,128,128]{2,1,0:T(8,128)(2,1)S(1)} %bitcast.14), custom_call_target="tpu_custom_call" | custom-call | bytes 6553600 | tf_op jit(solution)/shard_map/assemble/pallas_call | solution.py:48
  213.8 0.0 copy-start.3
  213.8 1.6 copy-done.3
  215.5 23.0 %pair_tiles.4 = f32[4,8,7,32,128]{4,3,2,1,0:T(8,128)} custom-call(s32[56]{0:T(128)} %slot_ref.11, bf16[1280,1280]{1,0:T(8,128)(2,1)} %copy-done.2, bf16[1280,1280]{1,0:T(8,128)(2,1)} %copy-done.3, bf16[1,3,1200,1200]{3,2,1,0:T(8,128)(2,1)} %wr_ref.5, bf16[1,3,1200,1200]{3,2,1,0:T(8,128)(2,1)} %wr_ref.5), custom_call_target="tpu_custom_call" | custom-call | flops 8388608000 | bytes 26214400 | tf_op jit(solution)/shard_map/pair_tiles/pallas_call | solution.py:132
  238.5 0.0 reduce-scatter.6.cloned.1.call-update
  238.5 0.0 reduce-scatter.8.cloned.1.call-start
  238.5 23.1 %pair_tiles.5 = f32[4,8,7,32,128]{4,3,2,1,0:T(8,128)} custom-call(s32[56]{0:T(128)} %slot_ref.11, bf16[1280,1280]{1,0:T(8,128)(2,1)} %copy-done.1, bf16[1280,1280]{1,0:T(8,128)(2,1)} %copy-done.3, bf16[1,3,1200,1200]{3,2,1,0:T(8,128)(2,1)} %wr_ref.5, bf16[1,3,1200,1200]{3,2,1,0:T(8,128)(2,1)} %wr_ref.5), custom_call_target="tpu_custom_call" | custom-call | flops 8388608000 | bytes 26214400 | tf_op jit(solution)/shard_map/pair_tiles/pallas_call | solution.py:132
  261.6 0.0 reduce-scatter.8.cloned.1.call-update
  261.7 25.5 %reduce-scatter.4.cloned.1.call-done = f32[1,7,32,128]{3,2,1,0:T(8,128)} async-done(((f32[32,7,32,128]{3,2,1,0:T(8,128)}), f32[1,7,32,128]{3,2,1,0:T(8,128)}) %reduce-scatter.4.cloned.1.call-update) | async-done | bytes 114704 | tf_op jit(solution)/shard_map/reduce_scatter | solution.py:177
  287.2 142.3 %reduce-scatter.6.cloned.1.call-done = f32[1,7,32,128]{3,2,1,0:T(8,128)} async-done(((f32[32,7,32,128]{3,2,1,0:T(8,128)}), f32[1,7,32,128]{3,2,1,0:T(8,128)}) %reduce-scatter.6.cloned.1.call-update) | async-done | bytes 114704 | tf_op jit(solution)/shard_map/reduce_scatter | solution.py:177
  429.5 141.5 %reduce-scatter.8.cloned.1.call-done = f32[1,7,32,128]{3,2,1,0:T(8,128)} async-done(((f32[32,7,32,128]{3,2,1,0:T(8,128)}), f32[1,7,32,128]{3,2,1,0:T(8,128)}) %reduce-scatter.8.cloned.1.call-update) | async-done | bytes 114704 | tf_op jit(solution)/shard_map/reduce_scatter | solution.py:177
  571.0 1.8 pad_maximum_fusion
  (3 shorter events, 0.0 us)
Async XLA Ops:
  12.8 53.4 %copy-start.4 = (s32[56]{0:T(128)S(1)}, s32[56]{0:T(128)}, u32[]{:S(2)}) copy-start(s32[56]{0:T(128)} %slot_ref.11) | copy-start | bytes 676
  62.6 46.9 %all-to-all-start.1 = ((bf16[8,7,128,128]{3,2,1,0:T(8,128)(2,1)}), bf16[8,7,128,128]{3,2,1,0:T(8,128)(2,1)S(1)}, u32[]{:S(2)}, u32[]{:S(2)}) async-start(bf16[8,7,128,128]{3,2,1,0:T(8,128)(2,1)} %get-tuple-element.7), calls=%async_computation.1 | async-start | bytes 3670016 | tf_op jit(solution)/shard_map/all_to_all | solution.py:165
  66.2 221.0 %reduce-scatter.4.cloned.1.call-start = ((), (), s32[]{:S(2)}) async-start(), calls=%async_computation.6 | async-start | bytes 3784704 | tf_op jit(solution)/shard_map/reduce_scatter | solution.py:177
  66.3 1.5 copy-start
  75.3 1.8 copy-start.2
  117.1 1.8 copy-start.1
  141.9 1.5 copy-start.6
  141.9 64.4 %copy-start.5 = (s32[56]{0:T(128)S(1)}, s32[56]{0:T(128)}, u32[]{:S(2)}) copy-start(s32[56]{0:T(128)} %slot_ref.11) | copy-start | bytes 676
  141.9 287.6 %reduce-scatter.6.cloned.1.call-start = ((), (), s32[]{:S(2)}) async-start(), calls=%async_computation.7 | async-start | bytes 3784704 | tf_op jit(solution)/shard_map/reduce_scatter | solution.py:177
  213.8 1.7 copy-start.3
  238.5 332.5 %reduce-scatter.8.cloned.1.call-start = ((), (), s32[]{:S(2)}) async-start(), calls=%async_computation.8 | async-start | bytes 3784704 | tf_op jit(solution)/shard_map/reduce_scatter | solution.py:177
Sparse Core Ops, SparseCore 0:
  142.0 145.1 reduce-scatter.3
  289.5 139.9 reduce-scatter.5
  431.8 139.1 reduce-scatter.7

commit v2 on v1

--- a/solution.py
+++ b/solution.py
@@ -9,7 +9,7 @@
 
 
 def assemble_kernel(v_width, blocks, slot_ref, packed_ref, full_ref):
-    n_slots, tile_len, _ = packed_ref.shape
+    n_blk, _, slot_dev, tile_len, _ = packed_ref.shape
     row_ids = lax.broadcasted_iota(jnp.int32, (tile_len, tile_len), 0)
     col_ids = lax.broadcasted_iota(jnp.int32, (tile_len, tile_len), 1)
 
@@ -25,7 +25,8 @@
             row_at = row_ids + first * tile_len
             col_at = col_ids + second * tile_len
             keep = jnp.logical_and(row_at < col_at, col_at < v_width)
-            tile = jnp.where(keep, packed_ref[slot].astype(jnp.float32), 0.0)
+            packed = packed_ref[lax.div(slot, slot_dev), 0, lax.rem(slot, slot_dev)]
+            tile = jnp.where(keep, packed.astype(jnp.float32), 0.0)
             mirror = tile.T
 
             @pl.when(first == second)
@@ -39,20 +40,25 @@
 
         return carry
 
-    lax.fori_loop(0, n_slots, place, 0)
-
-
-def assemble(slot_tile, packed, v_width, blocks):
-    tile_len = packed.shape[-1]
+    lax.fori_loop(0, n_blk * slot_dev, place, 0)
+
+
+def assemble(slot_tile, packed, which, v_width, blocks):
+    n_blk, _, slot_dev, tile_len, _ = packed.shape
     padded = blocks * tile_len
     return pl.pallas_call(
         functools.partial(assemble_kernel, v_width, blocks),
+        grid=(1,),
         out_shape=jax.ShapeDtypeStruct((padded, padded), packed.dtype),
         in_specs=[
             pl.BlockSpec(memory_space=pltpu.SMEM),
-            pl.BlockSpec(memory_space=pltpu.VMEM),
+            pl.BlockSpec(
+                (n_blk, 1, slot_dev, tile_len, tile_len),
+                lambda i: (0, which, 0, 0, 0),
+                pipeline_mode=pl.Buffered(1),
+            ),
         ],
-        out_specs=pl.BlockSpec(memory_space=pltpu.VMEM),
+        out_specs=pl.BlockSpec((padded, padded), lambda i: (0, 0), pipeline_mode=pl.Buffered(1)),
         compiler_params=pltpu.CompilerParams(vmem_limit_bytes=24 << 20),
         cost_estimate=pl.CostEstimate(
             flops=0, bytes_accessed=4 * padded * padded, transcendentals=0
@@ -62,13 +68,14 @@
 
 
 def pair_kernel(
-    blocks, n_slab, n_blk, slot_ref, left_ref, right_ref, wl_ref, wr_ref, out_ref, weights, differ
+    blocks, n_slab, n_blk, slot_ref, left_ref, right_ref, wl_ref, wr_ref, *rest
 ):
+    out_ref, weights, differ = rest[-3:]
     padded = left_ref.shape[0]
     v_width = wl_ref.shape[-1]
     tile_len = padded // blocks
     row_part = tile_len // n_slab
-    slot_dev = out_ref.shape[2]
+    slot_dev = out_ref.shape[3]
     pad = padded - v_width
     for half, ref in enumerate((wr_ref, wl_ref)):
         base = half * padded
@@ -103,24 +110,23 @@
             tile = differ[rows, cols] - differ[cols, rows].T
             for slab in range(n_slab):
                 part = tile[slab * row_part : (slab + 1) * row_part]
-                out_ref[slab, owner, place] = part
+                out_ref[slab, owner, 0, place] = part
 
         @pl.when(tile_id < 0)
         def _():
             for slab in range(n_slab):
-                out_ref[slab, owner, place] = jnp.zeros((row_part, tile_len), jnp.float32)
+                out_ref[slab, owner, 0, place] = jnp.zeros((row_part, tile_len), jnp.float32)
 
         return carry
 
     lax.fori_loop(0, n_blk * slot_dev, pack, 0)
 
 
-def pair_tiles(slot_tile, fulls, integrals, source, target, n_slab, n_blk, tile_len):
+def pair_tiles(slot_tile, fulls, integrals, source, target, pair, n_pair, held, n_slab, n_blk, tile_len):
     padded = fulls[0].shape[0]
     blocks = padded // tile_len
     v_width = integrals.shape[-1]
     slot_dev = slot_tile.shape[0] // n_blk
-    vmem = pl.BlockSpec(memory_space=pltpu.VMEM)
 
     def ints(which):
         return pl.BlockSpec((1, 1, v_width, v_width), lambda i: (0, which, 0, 0), pipeline_mode=pl.Buffered(1))
@@ -128,7 +134,9 @@
     def whole(shape):
         return pl.BlockSpec(shape, lambda i: (0,) * len(shape), pipeline_mode=pl.Buffered(1))
 
-    out_dims = (n_slab, n_blk, slot_dev, tile_len // n_slab, tile_len)
+    row_part = tile_len // n_slab
+    out_dims = (n_slab, n_blk, n_pair, slot_dev, row_part, tile_len)
+    more = [] if held is None else [held]
     return pl.pallas_call(
         functools.partial(pair_kernel, blocks, n_slab, n_blk),
         grid=(1,),
@@ -139,8 +147,14 @@
             whole((padded, padded)),
             ints(source),
             ints(target),
-        ],
-        out_specs=whole(out_dims),
+        ]
+        + [pl.BlockSpec(memory_space=pl.ANY) for _ in more],
+        out_specs=pl.BlockSpec(
+            (n_slab, n_blk, 1, slot_dev, row_part, tile_len),
+            lambda i: (0, 0, pair, 0, 0, 0),
+            pipeline_mode=pl.Buffered(1),
+        ),
+        input_output_aliases={5: 0} if more else {},
         scratch_shapes=[
             pltpu.VMEM((2 * padded, padded), fulls[0].dtype),
             pltpu.VMEM((padded, padded), jnp.float32),
@@ -150,7 +164,7 @@
             flops=4 * padded * padded * padded, bytes_accessed=16 * padded * padded, transcendentals=0
         ),
         name="pair_tiles",
-    )(slot_tile, fulls[source], fulls[target], integrals, integrals)
+    )(slot_tile, fulls[source], fulls[target], integrals, integrals, *more)
 
 
 def local(amplitudes, integrals, slot_tile):
@@ -160,24 +174,23 @@
     v_width = integrals.shape[-1]
     blocks = (v_width + tile_len - 1) // tile_len
     n_slots = slot_tile.shape[0]
-    fulls = []
-    for source in range(n_out):
-        moved = lax.all_to_all(
-            amplitudes[:, source], "blk", split_axis=0, concat_axis=0, tiled=True
+    row_part = tile_len // n_slab
+    last = n_out - 1
+    head = lax.all_to_all(amplitudes[:, :last], "blk", split_axis=0, concat_axis=0, tiled=True)
+    head, rest = lax.optimization_barrier((head, amplitudes[:, last:]))
+    tail = lax.all_to_all(rest, "blk", split_axis=0, concat_axis=0, tiled=True)
+    fulls = [assemble(slot_tile, head, source, v_width, blocks) for source in range(last)]
+    fulls.append(assemble(slot_tile, tail, 0, v_width, blocks))
+    pairs = [(source, target) for source in range(n_out) for target in range(source + 1, n_out)]
+    held = None
+    for source, target in sorted(pairs, key=lambda pair: pair[1]):
+        held = pair_tiles(
+            slot_tile, fulls, integrals, source, target, pairs.index((source, target)),
+            len(pairs), held, n_slab, n_blk, tile_len,
         )
-        packed = moved.reshape(n_slots, tile_len, tile_len)
-        fulls.append(assemble(slot_tile, packed, v_width, blocks))
-    shares = []
-    for target in range(n_out):
-        for source in range(target):
-            arranged = pair_tiles(
-                slot_tile, fulls, integrals, source, target, n_slab, n_blk, tile_len
-            )
-            arranged = arranged.reshape(n_slab * n_blk, slot_dev, tile_len // n_slab, tile_len)
-            share = lax.psum_scatter(arranged, ("slab", "blk"), scatter_dimension=0, tiled=True)
-            shares.append((source, target, share))
-    shares.sort(key=lambda item: item[:2])
-    return jnp.concatenate([item[2] for item in shares])
+    arranged = held.reshape(n_slab * n_blk, len(pairs), slot_dev, row_part, tile_len)
+    share = lax.psum_scatter(arranged, ("slab", "blk"), scatter_dimension=0, tiled=True)
+    return share.reshape(len(pairs), slot_dev, row_part, tile_len)
 
 
 def solution(mesh):

time: 580 us -> 356 us (0.61)
  waiting for transfers between devices: 342 us -> 225 us
  blocking collectives: 113 us -> 0 us
  starting transfers between devices: 3.72 us -> 9.99 us
    reduce_scatter x3 -> x1, waiting for transfers between devices: 309 us -> 145 us  [local(): lax.psum_scatter(arranged, ('slab', 'blk'), scatter_dimension=0, tiled=True)]
    all_to_all x2 -> x0, blocking collectives: 113 us -> none  [local(): lax.all_to_all(amplitudes[:, source], 'blk', split_axis=0, concat_axis=0,...]
    all_to_all x1 -> x2, waiting for transfers between devices: 32.5 us -> 79.8 us  [the longest x1 79.8 us: local(): lax.all_to_all(amplitudes[:, :last], 'blk', split_axis=0, concat_axis=0,...]
    slice x0 -> x2, local copies, waits for them, and re-layouts: none -> 7.35 us  [the longest x1 4.36 us: local(): amplitudes[:, :last]]
    all_to_all x1 -> x2, starting transfers between devices: 3.59 us -> 9.95 us  [the longest x1 6.35 us: local(): lax.all_to_all(amplitudes[:, :last], 'blk', split_axis=0, concat_axis=0,...]
    squeeze x1 -> x0, local copies, waits for them, and re-layouts: 6.29 us -> none  [local(): amplitudes[:, source]]
  transfers between devices with their start and end apart: 4 -> 3, of which waited for: 4 -> 2; matrix products, arithmetic and copies ran while one was open for 0% -> 1% of each run, Pallas kernels for 11% -> 11%
where the time goes in v2:
time: 356 us; the launch traced here: 355 us
  waiting for transfers between devices  225 us (63%)
  Pallas kernels  94 us (26%)
  between operations  13.5 us (4%)
  local copies, waits for them, and re-layouts  12.4 us (3%)
  starting transfers between devices  9.99 us (3%)
    reduce_scatter x1, waiting for transfers between devices, local(): lax.psum_scatter(arranged, ('slab', 'blk'), scatter_dimension=0, tiled=True)  145 us
    all_to_all x1, waiting for transfers between devices, local(): lax.all_to_all(amplitudes[:, :last], 'blk', split_axis=0, concat_axis=0,...  79.8 us
    pallas_call x3, Pallas kernels, pair_tiles(): pl.pallas_call(functools.partial(pair_kernel, blocks, n_slab, n_blk), gri...  69 us
    pallas_call x3, Pallas kernels, assemble(): pl.pallas_call(functools.partial(assemble_kernel, v_width, blocks), grid=...  25 us
  transfers between devices with their start and end apart: 3, of which 2 were waited for; matrix products, arithmetic and copies ran while one was open for 1% of the time, Pallas kernels for 11%

profile of v2, /device:TPU:0, one launch (start us, length us, event | category | flops | bytes accessed | tf_op | source)
XLA Modules:
  0.0 355.2 jit_solution(1717168203733353506)
XLA Ops:
  6.5 4.4 %slice.6 = bf16[8,2,7,128,128]{4,3,2,1,0:T(8,128)(2,1)} slice(bf16[8,3,7,128,128]{4,3,2,1,0:T(8,128)(2,1)} %param.3), slice={[0:8], [0:2], [0:7], [0:128], [0:128]} | slice | bytes 7340032 | tf_op jit(solution)/shard_map/slice | solution.py:179
  10.9 6.4 %all-to-all-start = ((bf16[8,2,7,128,128]{4,3,2,1,0:T(8,128)(2,1)}), bf16[8,2,7,128,128]{4,3,2,1,0:T(8,128)(2,1)}, u32[]{:S(2)}, u32[]{:S(2)}) async-start(bf16[8,2,7,128,128]{4,3,2,1,0:T(8,128)(2,1)} %slice.6), calls=%async_computation | async-start | bytes 7340032 | tf_op jit(solution)/shard_map/all_to_all | solution.py:179
  17.2 0.0 copy-start.3
  17.3 3.0 slice.7
  20.2 79.8 %all-to-all-done.packed_ref = bf16[8,2,7,128,128]{4,3,2,1,0:T(8,128)(2,1)} async-done(((bf16[8,2,7,128,128]{4,3,2,1,0:T(8,128)(2,1)}), bf16[8,2,7,128,128]{4,3,2,1,0:T(8,128)(2,1)}, u32[]{:S(2)}, u32[]{:S(2)}) %all-to-all-start) | async-done | bytes 3670048 | tf_op jit(solution)/shard_map/all_to_all | solution.py:179
  100.1 3.6 %all-to-all-start.1 = ((bf16[8,1,7,128,128]{4,3,2,1,0:T(8,128)(2,1)}), bf16[8,1,7,128,128]{4,3,2,1,0:T(8,128)(2,1)S(1)}, u32[]{:S(2)}, u32[]{:S(2)}) async-start(bf16[8,1,7,128,128]{4,3,2,1,0:T(8,128)(2,1)} %slice.7), calls=%async_computation.1 | async-start | bytes 3670016 | tf_op jit(solution)/shard_map/all_to_all | solution.py:181
  103.7 0.0 reduce-scatter.2.cloned.1.call-start
  103.7 0.0 copy-done.3
  103.8 8.7 %assemble.5.left_ref = bf16[1280,1280]{1,0:T(8,128)(2,1)S(1)} custom-call(s32[56]{0:T(128)S(1)} %copy-done.3, bf16[8,2,7,128,128]{4,3,2,1,0:T(8,128)(2,1)} %all-to-all-done.packed_ref), custom_call_target="tpu_custom_call" | custom-call | bytes 6553600 | tf_op jit(solution)/shard_map/assemble/pallas_call | solution.py:49
  112.4 0.0 copy-start.1
  112.4 1.6 copy-done.1
  114.1 8.7 %assemble.3.right_ref.left_ref = bf16[1280,1280]{1,0:T(8,128)(2,1)S(1)} custom-call(s32[56]{0:T(128)S(1)} %copy-done.3, bf16[8,2,7,128,128]{4,3,2,1,0:T(8,128)(2,1)} %all-to-all-done.packed_ref), custom_call_target="tpu_custom_call" | custom-call | bytes 6553600 | tf_op jit(solution)/shard_map/assemble/pallas_call | solution.py:49
  122.7 0.0 copy-start
  122.7 1.8 copy-done
  124.5 0.0 copy-start.4
  124.5 23.0 %pair_tiles.3.rest_0_ = f32[4,8,3,7,32,128]{5,4,3,2,1,0:T(8,128)} custom-call(s32[56]{0:T(128)} %slot_ref.11, bf16[1280,1280]{1,0:T(8,128)(2,1)} %copy-done.1, bf16[1280,1280]{1,0:T(8,128)(2,1)} %copy-done, bf16[1,3,1200,1200]{3,2,1,0:T(8,128)(2,1)} %wr_ref.5, bf16[1,3,1200,1200]{3,2,1,0:T(8,128)(2,1)} %wr_ref.5), custom_call_target="tpu_custom_call" | custom-call | flops 8388608000 | bytes 26214400 | tf_op jit(solution)/shard_map/pair_tiles/pallas_call | solution.py:140
  147.6 0.0 all-to-all-done.1.packed_ref
  147.6 0.0 copy-done.4
  147.6 7.7 %assemble.4.right_ref = bf16[1280,1280]{1,0:T(8,128)(2,1)S(1)} custom-call(s32[56]{0:T(128)S(1)} %copy-done.4, bf16[8,1,7,128,128]{4,3,2,1,0:T(8,128)(2,1)S(1)} %all-to-all-done.1.packed_ref), custom_call_target="tpu_custom_call" | custom-call | bytes 6553600 | tf_op jit(solution)/shard_map/assemble/pallas_call | solution.py:49
  155.3 0.0 copy-start.2
  155.3 1.6 copy-done.2
  156.9 22.9 %pair_tiles.4.rest_0_ = f32[4,8,3,7,32,128]{5,4,3,2,1,0:T(8,128)} custom-call(s32[56]{0:T(128)} %slot_ref.11, bf16[1280,1280]{1,0:T(8,128)(2,1)} %copy-done.1, bf16[1280,1280]{1,0:T(8,128)(2,1)} %copy-done.2, bf16[1,3,1200,1200]{3,2,1,0:T(8,128)(2,1)} %wr_ref.5, bf16[1,3,1200,1200]{3,2,1,0:T(8,128)(2,1)} %wr_ref.5, ...), custom_call_target="tpu_custom_call", output_to_operand_aliasing={{}: (5, {})} | custom-call | flops 8388608000 | bytes 26214400 | tf_op jit(solution)/shard_map/pair_tiles/pallas_call | solution.py:140
  179.8 23.0 %pair_tiles.5 = f32[4,8,3,7,32,128]{5,4,3,2,1,0:T(8,128)} custom-call(s32[56]{0:T(128)} %slot_ref.11, bf16[1280,1280]{1,0:T(8,128)(2,1)} %copy-done, bf16[1280,1280]{1,0:T(8,128)(2,1)} %copy-done.2, bf16[1,3,1200,1200]{3,2,1,0:T(8,128)(2,1)} %wr_ref.5, bf16[1,3,1200,1200]{3,2,1,0:T(8,128)(2,1)} %wr_ref.5, ...), custom_call_target="tpu_custom_call", output_to_operand_aliasing={{}: (5, {})} | custom-call | flops 8388608000 | bytes 26214400 | tf_op jit(solution)/shard_map/pair_tiles/pallas_call | solution.py:140
  202.9 0.0 reduce-scatter.2.cloned.1.call-update
  202.9 145.5 %reduce-scatter.2.cloned.1.call-done = f32[1,3,7,32,128]{4,3,2,1,0:T(8,128)} async-done(((f32[32,3,7,32,128]{4,3,2,1,0:T(8,128)}), f32[1,3,7,32,128]{4,3,2,1,0:T(8,128)}) %reduce-scatter.2.cloned.1.call-update) | async-done | bytes 344080 | tf_op jit(solution)/shard_map/reduce_scatter | solution.py:192
Async XLA Ops:
  10.9 89.2 %all-to-all-start = ((bf16[8,2,7,128,128]{4,3,2,1,0:T(8,128)(2,1)}), bf16[8,2,7,128,128]{4,3,2,1,0:T(8,128)(2,1)}, u32[]{:S(2)}, u32[]{:S(2)}) async-start(bf16[8,2,7,128,128]{4,3,2,1,0:T(8,128)(2,1)} %slice.6), calls=%async_computation | async-start | bytes 7340032 | tf_op jit(solution)/shard_map/all_to_all | solution.py:179
  17.2 86.5 %copy-start.3 = (s32[56]{0:T(128)S(1)}, s32[56]{0:T(128)}, u32[]{:S(2)}) copy-start(s32[56]{0:T(128)} %slot_ref.11) | copy-start | bytes 676
  100.1 47.5 %all-to-all-start.1 = ((bf16[8,1,7,128,128]{4,3,2,1,0:T(8,128)(2,1)}), bf16[8,1,7,128,128]{4,3,2,1,0:T(8,128)(2,1)S(1)}, u32[]{:S(2)}, u32[]{:S(2)}) async-start(bf16[8,1,7,128,128]{4,3,2,1,0:T(8,128)(2,1)} %slice.7), calls=%async_computation.1 | async-start | bytes 3670016 | tf_op jit(solution)/shard_map/all_to_all | solution.py:181
  103.7 244.7 %reduce-scatter.2.cloned.1.call-start = ((), (), s32[]{:S(2)}) async-start(), calls=%async_computation.3 | async-start | bytes 11354112 | tf_op jit(solution)/shard_map/reduce_scatter | solution.py:192
  112.4 1.7 copy-start.1
  122.7 1.8 copy-start
  124.5 23.0 %copy-start.4 = (s32[56]{0:T(128)S(1)}, s32[56]{0:T(128)}, u32[]{:S(2)}) copy-start(s32[56]{0:T(128)} %slot_ref.11) | copy-start | bytes 676
  155.3 1.7 copy-start.2
Sparse Core Ops, SparseCore 0:
  203.0 145.3 reduce-scatter.1
